TPU v7x, 32 devices: a whole 2x2x4 slice. The times are simulated.
32 devices in a mesh: row: 8 (over y, x, core), col: 4 (over z).
Axes of the slice: x: 2, y: 2, z: 4, core: 2. Of those that a mesh axis runs over, the one named last changes fastest.
Arguments:
- inputs: int32 [8, 128, 128], replicated, may hold values 0 or 1
- targets: int32 [8, 128, 128], replicated, may hold values 0 or 1
- initial_spikes: int32 [128, 128, 128], P(None, 'row'), may hold values 0 or 1
- w_in: bfloat16 [128, 128, 128], P(None, 'row'), may hold values from -0.5 to 0.5
- w_rec: bfloat16 [128, 128, 128, 128], P(None, 'col', 'row'), may hold values from -0.046875 to 0.046875
- w_out: bfloat16 [128, 128, 128], P('row'), may hold values from -0.046875 to 0.046875
- feedback: bfloat16 [128, 128, 128], P(None, 'row')
- adapt_gain: float32 [128, 128], P('row'), may hold values from 0.1 to 2
- adapt_decay: float32 [128, 128], P('row'), may hold values from 0.8 to 0.99
Outputs:
- readout: float32 [8, 128, 128], replicated
- grad_clipped: float32 [128, 128, 128, 128], P(None, 'col', 'row')
All inputs are finite; a program needn't handle non-finite values. No bound on the sum of `initial_spikes` on one device may be relied on, other than what follows from the above.
Results may differ from a plain program's by a relative error of at most 0.0015.
Values may be sent and summed in bfloat16 or wider, within the bound.
No kernel may reach another device: no remote copies, remote signals or barrier semaphores. Data moves between devices by JAX's collectives and lax.ppermute only.
A program may use at most 128 MiB of HBM per device.

v0:
```python
import jax
import jax.numpy as jnp
from jax import lax
from jax.sharding import PartitionSpec as P

NA = 128
NB = 128
cellular_leak_multiplier = 0.8
readout_decay = 0.8


def body(inputs, targets, initial_spikes, w_in, w_rec, w_out, feedback, adapt_gain, adapt_decay):
    steps_count, batch, channels = inputs.shape
    own_cols = w_rec.shape[1]
    rows_loc = w_rec.shape[2]
    entire_column_set = w_rec.shape[3]
    col_start = lax.axis_index("col") * own_cols
    rows_all = steps_count * batch

    def own_part(array, axis_dim):
        return lax.dynamic_slice_in_dim(array, col_start, own_cols, axis_dim)

    def select_cols(array, axis_dim):
        return own_part(array, axis_dim)

    def combine_currents(partial_value):
        return lax.psum_scatter(partial_value, "col", scatter_dimension=2, tiled=True)

    weights = w_rec.reshape(w_rec.shape[0] * own_cols, rows_loc * entire_column_set)
    w_in_loc = select_cols(w_in, 2)
    state_cols = w_in_loc.shape[2]
    external = jnp.dot(
        inputs.reshape(rows_all, channels).astype(jnp.bfloat16),
        w_in_loc.reshape(channels, -1),
        preferred_element_type=jnp.float32,
    ).reshape(steps_count, batch, rows_loc, state_cols)
    coupling_magnitude = select_cols(adapt_gain, 1)
    retention = select_cols(adapt_decay, 1)
    start_spikes = select_cols(initial_spikes, 2).astype(jnp.bfloat16)

    def advance(state, drive_now):
        pulse_output, cellular_charge, barrier_shift_amount, sender_trace = state
        arrivals = lax.all_gather(pulse_output, "row", axis=1, tiled=True).reshape(batch, -1)
        sender_trace = cellular_leak_multiplier * sender_trace + arrivals.astype(jnp.float32)
        partial_value = jnp.dot(arrivals, weights, preferred_element_type=jnp.float32).reshape(
            batch, rows_loc, entire_column_set
        )
        current = drive_now + combine_currents(partial_value)
        spike_float = pulse_output.astype(jnp.float32)
        cellular_charge = cellular_leak_multiplier * cellular_charge + current - spike_float
        barrier_shift_amount = retention * barrier_shift_amount + spike_float
        present_emission_frequency = jax.nn.sigmoid(
            cellular_charge - 1.0 - coupling_magnitude * barrier_shift_amount
        )
        surrogate_slope = present_emission_frequency * (1.0 - present_emission_frequency)
        pulse_output = present_emission_frequency.astype(jnp.bfloat16)
        return (
            (pulse_output, cellular_charge, barrier_shift_amount, sender_trace),
            (sender_trace.astype(jnp.bfloat16), surrogate_slope, pulse_output),
        )

    zeros = jnp.zeros((batch, rows_loc, state_cols), jnp.float32)
    trace_zero = jnp.zeros((batch, weights.shape[0]), jnp.float32)
    _, (traces, slopes, spikes) = lax.scan(
        advance, (start_spikes, zeros, zeros, trace_zero), external
    )
    readout_loc = own_part(w_out, 1).reshape(rows_loc * own_cols, -1)
    projected = lax.psum(
        jnp.dot(spikes.reshape(rows_all, -1), readout_loc, preferred_element_type=jnp.float32),
        ("row", "col"),
    )
    outputs_n = readout_loc.shape[1]
    projected = projected.reshape(steps_count, batch, outputs_n)

    def smooth(level, incoming):
        level = readout_decay * level + incoming
        return (level, level)

    _, readout = lax.scan(smooth, jnp.zeros((batch, outputs_n), jnp.float32), projected)
    errors = (jax.nn.sigmoid(readout) - targets.astype(jnp.float32)).reshape(rows_all, outputs_n)
    err_high = errors.astype(jnp.bfloat16)
    err_low = (errors - err_high.astype(jnp.float32)).astype(jnp.bfloat16)
    feedback_loc = select_cols(feedback, 2).reshape(outputs_n, -1)
    signal = jnp.dot(err_high, feedback_loc, preferred_element_type=jnp.float32) + jnp.dot(
        err_low, feedback_loc, preferred_element_type=jnp.float32
    )
    signal = signal.reshape(steps_count, batch, rows_loc, state_cols)
    weighted = signal * slopes
    decays = retention - slopes * coupling_magnitude

    def backward(carried, inputs_now):
        weighted_now, decay_now = inputs_now
        return (weighted_now + decay_now * carried, carried)

    _, future = lax.scan(backward, zeros, (weighted, decays), reverse=True)
    factors = (weighted - coupling_magnitude * slopes * future).astype(jnp.bfloat16)
    traces_flat = traces.reshape(rows_all, -1)
    pieces = lax.all_gather(
        factors.reshape(rows_all, rows_loc, state_cols), "col", axis=2, tiled=True
    )
    product = lax.dot_general(
        traces_flat,
        pieces.reshape(rows_all, -1),
        (((0,), (0,)), ((), ())),
        preferred_element_type=jnp.float32,
    )
    grad = product.reshape(-1, rows_loc, pieces.shape[2])
    squares = lax.psum(jnp.sum(grad * grad), ("row", "col"))
    clip_factor = jnp.minimum(1.0, NA * NB / 16.0 / jnp.sqrt(squares + 1e-06))
    return (readout, (grad * clip_factor).reshape(w_rec.shape))


def solution(mesh):
    return jax.shard_map(
        body,
        mesh=mesh,
        in_specs=(
            P(),
            P(),
            P(None, "row", None),
            P(None, "row", None),
            P(None, "col", "row", None),
            P("row", None, None),
            P(None, "row", None),
            P("row", None),
            P("row", None),
        ),
        out_specs=(P(), P(None, "col", "row", None)),
        check_vma=False,
    )
```

profile of v0, /device:TPU:0, one launch (start us, length us, event | category | flops | bytes accessed | tf_op | source)
XLA Modules:
  0.0 1113.9 jit_solution(2757752575109716151)
XLA Ops:
  15.9 17.2 %copy.96 = bf16[512,8,16,128]{3,1,2,0:T(8,128)(2,1)} copy(bf16[512,8,16,128]{3,2,1,0:T(8,128)(2,1)} %bitcast.115) | data formatting | bytes 33554432
  33.1 21.2 %copy.58 = bf16[4096,2048]{0,1:T(8,128)(2,1)} copy(bf16[4096,2048]{1,0:T(8,128)(2,1)} %bitcast.112) | data formatting | bytes 33554432
  55.9 592.0 %while.55 = (s32[]{:T(128)}, bf16[128,16,32]{0,2,1:T(8,128)(2,1)S(1)}, f32[128,16,32]{0,2,1:T(8,128)S(1)}, f32[128,16,32]{0,2,1:T(8,128)S(1)}, f32[128,4096]{0,1...) while((s32[]{:T(128)}, ...), condition=%wide.region_2.3_spmd.clone, body=%wide.region_0.2_spmd.clone.sunk | while | flops 2151677952 | bytes 45881672 | solution.py:64
  56.7 28.0 %all-gather.5.cloned.1.call-done = bf16[128,128,32]{0,2,1:T(8,128)(2,1)} async-done(((bf16[128,16,32]{0,2,1:T(8,128)(2,1)}), bf16[128,128,32]{0,2,1:T(8,128)(2,1)}) %all-gather.5.cloned.1.call-update) | async-done | bytes 1048592 | tf_op jit(solution)/shard_map/while/body/eval_jaxpr/all_gather | solution.py:43
  84.7 11.6 %fusion.29 = f32[128,16,128]{0,2,1:T(8,128)} fusion(bf16[128,4096,1]{0,1,2:T(8,128)(2,1)} %bitcast.111, bf16[16,128,4096]{2,1,0:T(8,128)(2,1)} %bitcast.109), kind=kOutput, calls=%fused_computation.43.clone.1 | convolution fusion | flops 2147483648 | bytes 18874368 | tf_op jit(solution)/shard_map/while/body/eval_jaxpr/dot_general | solution.py:45
  101.7 22.1 %reduce-scatter.2.cloned.1.call-done = f32[128,16,32]{0,2,1:T(8,128)} async-done(((f32[128,16,128]{0,2,1:T(8,128)}), f32[128,16,32]{0,2,1:T(8,128)}) %reduce-scatter.2.cloned.1.call-update) | async-done | bytes 262160 | tf_op jit(solution)/shard_map/while/body/eval_jaxpr/reduce_scatter | solution.py:27
  134.5 23.8 %all-gather.5.cloned.1.call-done = bf16[128,128,32]{0,2,1:T(8,128)(2,1)} async-done(((bf16[128,16,32]{0,2,1:T(8,128)(2,1)}), bf16[128,128,32]{0,2,1:T(8,128)(2,1)}) %all-gather.5.cloned.1.call-update) | async-done | bytes 1048592 | tf_op jit(solution)/shard_map/while/body/eval_jaxpr/all_gather | solution.py:43
  158.3 11.6 %fusion.29 = f32[128,16,128]{0,2,1:T(8,128)} fusion(bf16[128,4096,1]{0,1,2:T(8,128)(2,1)} %bitcast.111, bf16[16,128,4096]{2,1,0:T(8,128)(2,1)} %bitcast.109), kind=kOutput, calls=%fused_computation.43.clone.1 | convolution fusion | flops 2147483648 | bytes 18874368 | tf_op jit(solution)/shard_map/while/body/eval_jaxpr/dot_general | solution.py:45
  176.8 20.5 %reduce-scatter.2.cloned.1.call-done = f32[128,16,32]{0,2,1:T(8,128)} async-done(((f32[128,16,128]{0,2,1:T(8,128)}), f32[128,16,32]{0,2,1:T(8,128)}) %reduce-scatter.2.cloned.1.call-update) | async-done | bytes 262160 | tf_op jit(solution)/shard_map/while/body/eval_jaxpr/reduce_scatter | solution.py:27
  207.9 23.6 %all-gather.5.cloned.1.call-done = bf16[128,128,32]{0,2,1:T(8,128)(2,1)} async-done(((bf16[128,16,32]{0,2,1:T(8,128)(2,1)}), bf16[128,128,32]{0,2,1:T(8,128)(2,1)}) %all-gather.5.cloned.1.call-update) | async-done | bytes 1048592 | tf_op jit(solution)/shard_map/while/body/eval_jaxpr/all_gather | solution.py:43
  231.5 11.6 %fusion.29 = f32[128,16,128]{0,2,1:T(8,128)} fusion(bf16[128,4096,1]{0,1,2:T(8,128)(2,1)} %bitcast.111, bf16[16,128,4096]{2,1,0:T(8,128)(2,1)} %bitcast.109), kind=kOutput, calls=%fused_computation.43.clone.1 | convolution fusion | flops 2147483648 | bytes 18874368 | tf_op jit(solution)/shard_map/while/body/eval_jaxpr/dot_general | solution.py:45
  250.1 20.5 %reduce-scatter.2.cloned.1.call-done = f32[128,16,32]{0,2,1:T(8,128)} async-done(((f32[128,16,128]{0,2,1:T(8,128)}), f32[128,16,32]{0,2,1:T(8,128)}) %reduce-scatter.2.cloned.1.call-update) | async-done | bytes 262160 | tf_op jit(solution)/shard_map/while/body/eval_jaxpr/reduce_scatter | solution.py:27
  281.2 23.8 %all-gather.5.cloned.1.call-done = bf16[128,128,32]{0,2,1:T(8,128)(2,1)} async-done(((bf16[128,16,32]{0,2,1:T(8,128)(2,1)}), bf16[128,128,32]{0,2,1:T(8,128)(2,1)}) %all-gather.5.cloned.1.call-update) | async-done | bytes 1048592 | tf_op jit(solution)/shard_map/while/body/eval_jaxpr/all_gather | solution.py:43
  305.1 11.6 %fusion.29 = f32[128,16,128]{0,2,1:T(8,128)} fusion(bf16[128,4096,1]{0,1,2:T(8,128)(2,1)} %bitcast.111, bf16[16,128,4096]{2,1,0:T(8,128)(2,1)} %bitcast.109), kind=kOutput, calls=%fused_computation.43.clone.1 | convolution fusion | flops 2147483648 | bytes 18874368 | tf_op jit(solution)/shard_map/while/body/eval_jaxpr/dot_general | solution.py:45
  323.6 20.5 %reduce-scatter.2.cloned.1.call-done = f32[128,16,32]{0,2,1:T(8,128)} async-done(((f32[128,16,128]{0,2,1:T(8,128)}), f32[128,16,32]{0,2,1:T(8,128)}) %reduce-scatter.2.cloned.1.call-update) | async-done | bytes 262160 | tf_op jit(solution)/shard_map/while/body/eval_jaxpr/reduce_scatter | solution.py:27
  354.8 23.8 %all-gather.5.cloned.1.call-done = bf16[128,128,32]{0,2,1:T(8,128)(2,1)} async-done(((bf16[128,16,32]{0,2,1:T(8,128)(2,1)}), bf16[128,128,32]{0,2,1:T(8,128)(2,1)}) %all-gather.5.cloned.1.call-update) | async-done | bytes 1048592 | tf_op jit(solution)/shard_map/while/body/eval_jaxpr/all_gather | solution.py:43
  378.6 11.6 %fusion.29 = f32[128,16,128]{0,2,1:T(8,128)} fusion(bf16[128,4096,1]{0,1,2:T(8,128)(2,1)} %bitcast.111, bf16[16,128,4096]{2,1,0:T(8,128)(2,1)} %bitcast.109), kind=kOutput, calls=%fused_computation.43.clone.1 | convolution fusion | flops 2147483648 | bytes 18874368 | tf_op jit(solution)/shard_map/while/body/eval_jaxpr/dot_general | solution.py:45
  397.2 20.5 %reduce-scatter.2.cloned.1.call-done = f32[128,16,32]{0,2,1:T(8,128)} async-done(((f32[128,16,128]{0,2,1:T(8,128)}), f32[128,16,32]{0,2,1:T(8,128)}) %reduce-scatter.2.cloned.1.call-update) | async-done | bytes 262160 | tf_op jit(solution)/shard_map/while/body/eval_jaxpr/reduce_scatter | solution.py:27
  428.3 23.8 %all-gather.5.cloned.1.call-done = bf16[128,128,32]{0,2,1:T(8,128)(2,1)} async-done(((bf16[128,16,32]{0,2,1:T(8,128)(2,1)}), bf16[128,128,32]{0,2,1:T(8,128)(2,1)}) %all-gather.5.cloned.1.call-update) | async-done | bytes 1048592 | tf_op jit(solution)/shard_map/while/body/eval_jaxpr/all_gather | solution.py:43
  470.7 20.5 %reduce-scatter.2.cloned.1.call-done = f32[128,16,32]{0,2,1:T(8,128)} async-done(((f32[128,16,128]{0,2,1:T(8,128)}), f32[128,16,32]{0,2,1:T(8,128)}) %reduce-scatter.2.cloned.1.call-update) | async-done | bytes 262160 | tf_op jit(solution)/shard_map/while/body/eval_jaxpr/reduce_scatter | solution.py:27
  501.9 23.8 %all-gather.5.cloned.1.call-done = bf16[128,128,32]{0,2,1:T(8,128)(2,1)} async-done(((bf16[128,16,32]{0,2,1:T(8,128)(2,1)}), bf16[128,128,32]{0,2,1:T(8,128)(2,1)}) %all-gather.5.cloned.1.call-update) | async-done | bytes 1048592 | tf_op jit(solution)/shard_map/while/body/eval_jaxpr/all_gather | solution.py:43
  525.7 11.6 %fusion.29 = f32[128,16,128]{0,2,1:T(8,128)} fusion(bf16[128,4096,1]{0,1,2:T(8,128)(2,1)} %bitcast.111, bf16[16,128,4096]{2,1,0:T(8,128)(2,1)} %bitcast.109), kind=kOutput, calls=%fused_computation.43.clone.1 | convolution fusion | flops 2147483648 | bytes 18874368 | tf_op jit(solution)/shard_map/while/body/eval_jaxpr/dot_general | solution.py:45
  544.2 20.6 %reduce-scatter.2.cloned.1.call-done = f32[128,16,32]{0,2,1:T(8,128)} async-done(((f32[128,16,128]{0,2,1:T(8,128)}), f32[128,16,32]{0,2,1:T(8,128)}) %reduce-scatter.2.cloned.1.call-update) | async-done | bytes 262160 | tf_op jit(solution)/shard_map/while/body/eval_jaxpr/reduce_scatter | solution.py:27
  575.4 23.6 %all-gather.5.cloned.1.call-done = bf16[128,128,32]{0,2,1:T(8,128)(2,1)} async-done(((bf16[128,16,32]{0,2,1:T(8,128)(2,1)}), bf16[128,128,32]{0,2,1:T(8,128)(2,1)}) %all-gather.5.cloned.1.call-update) | async-done | bytes 1048592 | tf_op jit(solution)/shard_map/while/body/eval_jaxpr/all_gather | solution.py:43
  617.5 20.5 %reduce-scatter.2.cloned.1.call-done = f32[128,16,32]{0,2,1:T(8,128)} async-done(((f32[128,16,128]{0,2,1:T(8,128)}), f32[128,16,32]{0,2,1:T(8,128)}) %reduce-scatter.2.cloned.1.call-update) | async-done | bytes 262160 | tf_op jit(solution)/shard_map/while/body/eval_jaxpr/reduce_scatter | solution.py:27
  651.9 129.3 %all-reduce.2.cloned.1.call-done = f32[8,128,128]{2,1,0:T(8,128)} async-done(((f32[8,128,128]{2,1,0:T(8,128)}), f32[8,128,128]{2,1,0:T(8,128)}) %all-reduce.2.cloned.1.call-update) | async-done | bytes 524304 | tf_op jit(solution)/shard_map/psum | solution.py:68
  798.2 112.8 %while.57 = (s32[]{:T(128)}, f32[128,16,32]{2,1,0:T(8,128)}, f32[8,128,16,32]{1,0,3,2:T(8,128)}, f32[8,128,16,32]{1,0,3,2:T(8,128)}, f32[8,128,16,32]{1,0,3,2:T(8,128)}, /*index=5*/s32[]{:T(128)}, s32[]{:T(128)}, s32[]{:T(128)}) while((s32[]{:T(128)}, f32[128,16,32]{2,1,0:T(8,128)}, f32[8,128,16,32]{1,0,3,2:T(8,128)}, ...), condition=%wide.region_7.8_spmd.clone, body=%wide.region_6.7_spmd.clone.sunk | while | flops 196612 | bytes 4456571 | solution.py:95
  915.5 79.8 %all-gather.3.cloned.1.call-done = bf16[1024,16,128]{0,2,1:T(8,128)(2,1)} async-done(((bf16[1024,16,32]{0,2,1:T(8,128)(2,1)}), bf16[1024,16,128]{0,2,1:T(8,128)(2,1)}) %all-gather.3.cloned.1.call-update) | async-done | bytes 4194320 | tf_op jit(solution)/shard_map/all_gather | solution.py:98
  995.3 26.1 %multiply_reduce_fusion = (f32[]{:T(128)}, f32[4096,16,128]{2,0,1:T(8,128)}) fusion(bf16[1024,4096,1]{1,0,2:T(8,128)(2,1)} %bitcast.128, bf16[1024,16,128]{0,2,1:T(8,128)(2,1)} %all-gather.3.cloned.1.call-done), kind=kOutput, calls=%fused_computation.22 | convolution fusion | flops 17196646400 | bytes 46137348 | tf_op jit(solution)/shard_map/dot_general | solution.py:101
  1021.4 39.1 %psum.15 = f32[]{:T(128)} all-reduce(f32[]{:T(128)} %get-tuple-element.484), channel_id=1, replica_groups=mesh['row'=8,'col'=4] {'row','col'}, use_global_device_ids=true, to_apply=%region_9.10 | all-reduce | flops 1 | bytes 8 | tf_op jit(solution)/shard_map/psum | solution.py:108
  1061.2 11.9 %broadcast_multiply_fusion = f32[4096,16,128]{2,0,1:T(8,128)S(1)} fusion(f32[4096,16,128]{2,0,1:T(8,128)} %get-tuple-element.485, f32[]{:T(128)S(6)} %min.3), kind=kLoop, calls=%fused_computation.24 | loop fusion | flops 8388608 | bytes 67108864 | tf_op jit(solution)/shard_map/mul | solution.py:110
  1073.1 33.7 %copy.69 = f32[128,32,16,128]{3,2,1,0:T(8,128)} copy(f32[128,32,16,128]{3,1,0,2:T(8,128)S(1)} %bitcast.110) | data formatting | bytes 67108864
  (246 shorter events, 316.2 us)
Async XLA Ops:
  8.0 2.8 copy-start
  33.1 21.2 %copy-start.9 = (f32[16,128]{1,0:T(8,128)S(1)}, f32[16,128]{1,0:T(8,128)}, u32[]{:S(2)}) copy-start(f32[16,128]{1,0:T(8,128)} %param.23) | copy-start | bytes 24580
  33.1 21.2 %copy-start.10 = (f32[16,128]{1,0:T(8,128)S(1)}, f32[16,128]{1,0:T(8,128)}, u32[]{:S(2)}) copy-start(f32[16,128]{1,0:T(8,128)} %param.22) | copy-start | bytes 24580
  55.9 28.8 %all-gather.5.cloned.1.call-start = ((), (), s32[]{:S(2)}) async-start(), calls=%async_computation.3 | async-start | bytes 1179648 | tf_op jit(solution)/shard_map/while/body/eval_jaxpr/all_gather | solution.py:43
  56.6 67.2 %reduce-scatter.2.cloned.1.call-start = ((), (), s32[]{:S(2)}) async-start(), calls=%async_computation.4 | async-start | bytes 1310720 | tf_op jit(solution)/shard_map/while/body/eval_jaxpr/reduce_scatter | solution.py:27
  100.1 23.7 %copy-start.5 = (bf16[128,16,32]{0,2,1:T(8,128)(2,1)S(1)}, bf16[128,16,32]{0,2,1:T(8,128)(2,1)}, u32[]{:S(2)}) copy-start(bf16[128,16,32]{0,2,1:T(8,128)(2,1)} %copy-done.4) | copy-start | bytes 393220 | tf_op jit(solution)/shard_map/while
  133.7 24.6 %all-gather.5.cloned.1.call-start = ((), (), s32[]{:S(2)}) async-start(), calls=%async_computation.3 | async-start | bytes 1179648 | tf_op jit(solution)/shard_map/while/body/eval_jaxpr/all_gather | solution.py:43
  134.4 62.9 %reduce-scatter.2.cloned.1.call-start = ((), (), s32[]{:S(2)}) async-start(), calls=%async_computation.4 | async-start | bytes 1310720 | tf_op jit(solution)/shard_map/while/body/eval_jaxpr/reduce_scatter | solution.py:27
  175.2 22.2 %copy-start.5 = (bf16[128,16,32]{0,2,1:T(8,128)(2,1)S(1)}, bf16[128,16,32]{0,2,1:T(8,128)(2,1)}, u32[]{:S(2)}) copy-start(bf16[128,16,32]{0,2,1:T(8,128)(2,1)} %copy-done.4) | copy-start | bytes 393220 | tf_op jit(solution)/shard_map/while
  207.2 24.3 %all-gather.5.cloned.1.call-start = ((), (), s32[]{:S(2)}) async-start(), calls=%async_computation.3 | async-start | bytes 1179648 | tf_op jit(solution)/shard_map/while/body/eval_jaxpr/all_gather | solution.py:43
  207.9 62.7 %reduce-scatter.2.cloned.1.call-start = ((), (), s32[]{:S(2)}) async-start(), calls=%async_computation.4 | async-start | bytes 1310720 | tf_op jit(solution)/shard_map/while/body/eval_jaxpr/reduce_scatter | solution.py:27
  248.4 22.2 %copy-start.5 = (bf16[128,16,32]{0,2,1:T(8,128)(2,1)S(1)}, bf16[128,16,32]{0,2,1:T(8,128)(2,1)}, u32[]{:S(2)}) copy-start(bf16[128,16,32]{0,2,1:T(8,128)(2,1)} %copy-done.4) | copy-start | bytes 393220 | tf_op jit(solution)/shard_map/while
  280.5 24.6 %all-gather.5.cloned.1.call-start = ((), (), s32[]{:S(2)}) async-start(), calls=%async_computation.3 | async-start | bytes 1179648 | tf_op jit(solution)/shard_map/while/body/eval_jaxpr/all_gather | solution.py:43
  281.2 62.9 %reduce-scatter.2.cloned.1.call-start = ((), (), s32[]{:S(2)}) async-start(), calls=%async_computation.4 | async-start | bytes 1310720 | tf_op jit(solution)/shard_map/while/body/eval_jaxpr/reduce_scatter | solution.py:27
  322.0 22.2 %copy-start.5 = (bf16[128,16,32]{0,2,1:T(8,128)(2,1)S(1)}, bf16[128,16,32]{0,2,1:T(8,128)(2,1)}, u32[]{:S(2)}) copy-start(bf16[128,16,32]{0,2,1:T(8,128)(2,1)} %copy-done.4) | copy-start | bytes 393220 | tf_op jit(solution)/shard_map/while
  354.0 24.6 %all-gather.5.cloned.1.call-start = ((), (), s32[]{:S(2)}) async-start(), calls=%async_computation.3 | async-start | bytes 1179648 | tf_op jit(solution)/shard_map/while/body/eval_jaxpr/all_gather | solution.py:43
  354.7 62.9 %reduce-scatter.2.cloned.1.call-start = ((), (), s32[]{:S(2)}) async-start(), calls=%async_computation.4 | async-start | bytes 1310720 | tf_op jit(solution)/shard_map/while/body/eval_jaxpr/reduce_scatter | solution.py:27
  395.5 22.2 %copy-start.5 = (bf16[128,16,32]{0,2,1:T(8,128)(2,1)S(1)}, bf16[128,16,32]{0,2,1:T(8,128)(2,1)}, u32[]{:S(2)}) copy-start(bf16[128,16,32]{0,2,1:T(8,128)(2,1)} %copy-done.4) | copy-start | bytes 393220 | tf_op jit(solution)/shard_map/while
  427.6 24.6 %all-gather.5.cloned.1.call-start = ((), (), s32[]{:S(2)}) async-start(), calls=%async_computation.3 | async-start | bytes 1179648 | tf_op jit(solution)/shard_map/while/body/eval_jaxpr/all_gather | solution.py:43
  428.3 62.9 %reduce-scatter.2.cloned.1.call-start = ((), (), s32[]{:S(2)}) async-start(), calls=%async_computation.4 | async-start | bytes 1310720 | tf_op jit(solution)/shard_map/while/body/eval_jaxpr/reduce_scatter | solution.py:27
  469.1 22.2 %copy-start.5 = (bf16[128,16,32]{0,2,1:T(8,128)(2,1)S(1)}, bf16[128,16,32]{0,2,1:T(8,128)(2,1)}, u32[]{:S(2)}) copy-start(bf16[128,16,32]{0,2,1:T(8,128)(2,1)} %copy-done.4) | copy-start | bytes 393220 | tf_op jit(solution)/shard_map/while
  501.1 24.6 %all-gather.5.cloned.1.call-start = ((), (), s32[]{:S(2)}) async-start(), calls=%async_computation.3 | async-start | bytes 1179648 | tf_op jit(solution)/shard_map/while/body/eval_jaxpr/all_gather | solution.py:43
  501.8 62.9 %reduce-scatter.2.cloned.1.call-start = ((), (), s32[]{:S(2)}) async-start(), calls=%async_computation.4 | async-start | bytes 1310720 | tf_op jit(solution)/shard_map/while/body/eval_jaxpr/reduce_scatter | solution.py:27
  542.6 22.2 %copy-start.5 = (bf16[128,16,32]{0,2,1:T(8,128)(2,1)S(1)}, bf16[128,16,32]{0,2,1:T(8,128)(2,1)}, u32[]{:S(2)}) copy-start(bf16[128,16,32]{0,2,1:T(8,128)(2,1)} %copy-done.4) | copy-start | bytes 393220 | tf_op jit(solution)/shard_map/while
  574.7 24.3 %all-gather.5.cloned.1.call-start = ((), (), s32[]{:S(2)}) async-start(), calls=%async_computation.3 | async-start | bytes 1179648 | tf_op jit(solution)/shard_map/while/body/eval_jaxpr/all_gather | solution.py:43
  575.3 62.7 %reduce-scatter.2.cloned.1.call-start = ((), (), s32[]{:S(2)}) async-start(), calls=%async_computation.4 | async-start | bytes 1310720 | tf_op jit(solution)/shard_map/while/body/eval_jaxpr/reduce_scatter | solution.py:27
  615.9 22.2 %copy-start.5 = (bf16[128,16,32]{0,2,1:T(8,128)(2,1)S(1)}, bf16[128,16,32]{0,2,1:T(8,128)(2,1)}, u32[]{:S(2)}) copy-start(bf16[128,16,32]{0,2,1:T(8,128)(2,1)} %copy-done.4) | copy-start | bytes 393220 | tf_op jit(solution)/shard_map/while
  647.9 133.3 %all-reduce.2.cloned.1.call-start = ((), (), s32[]{:S(2)}) async-start(), calls=%async_computation.1 | async-start | bytes 1048576 | tf_op jit(solution)/shard_map/psum | solution.py:68
  649.8 138.4 %copy-start.6 = (s32[8,128,128]{2,1,0:T(8,128)S(1)}, s32[8,128,128]{2,1,0:T(8,128)}, u32[]{:S(2)}) copy-start(s32[8,128,128]{2,1,0:T(8,128)} %param.16) | copy-start | bytes 1572868
  651.2 344.1 %all-gather.3.cloned.1.call-start = ((), (), s32[]{:S(2)}) async-start(), calls=%async_computation.2 | async-start | bytes 5242880 | tf_op jit(solution)/shard_map/all_gather | solution.py:98
  791.2 2.2 copy-start.3
  1073.1 33.7 %copy-start.1 = (s32[128,16,128]{2,1,0:T(8,128)S(1)}, s32[128,16,128]{2,1,0:T(8,128)}, u32[]{:S(2)}) copy-start(s32[128,16,128]{2,1,0:T(8,128)} %param.17) | copy-start | bytes 3145732
  (18 other events, 23.8 us)
Sparse Core Ops, SparseCore 0:
  58.6 26.0 all-gather.4
  96.5 27.2 reduce-scatter.1
  136.4 21.8 all-gather.4
  170.0 27.2 reduce-scatter.1
  209.6 21.8 all-gather.4
  243.3 27.2 reduce-scatter.1
  283.1 21.8 all-gather.4
  316.8 27.2 reduce-scatter.1
  356.7 21.8 all-gather.4
  390.4 27.2 reduce-scatter.1
  430.2 21.8 all-gather.4
  463.9 27.2 reduce-scatter.1
  503.8 21.8 all-gather.4
  537.5 27.2 reduce-scatter.1
  577.0 21.8 all-gather.4
  610.7 27.2 reduce-scatter.1
Sparse Core Ops, SparseCore 1:
  654.2 126.9 all-reduce.1
  915.6 79.7 all-gather.2
where the time goes:
time: 1120 us; the launch traced here: 1110 us
  waiting for transfers between devices  570 us (51%)
  local copies, waits for them, and re-layouts  279 us (25%)
  matrix products  122 us (11%)
  other arithmetic  87.2 us (8%)
  blocking collectives  39.1 us (3%)
  between operations  16 us (1%)
    all_gather x8, waiting for transfers between devices, advance(): lax.all_gather(pulse_output, 'row', axis=1, tiled=True).reshape(batch, -1)  194 us
    reduce_scatter x8, waiting for transfers between devices, combine_currents(): lax.psum_scatter(partial_value, 'col', scatter_dimension=2, tiled=True)  166 us
    dynamic_update_slice x40, local copies, waits for them, and re-layouts, body(): lax.scan(advance, (start_spikes, zeros, zeros, trace_zero), external)  140 us
    psum x1, waiting for transfers between devices, body(): lax.psum(jnp.dot(spikes.reshape(rows_all, -1), readout_loc, preferred_ele...  129 us
    dot_general x8, matrix products, advance(): jnp.dot(arrivals, weights, preferred_element_type=jnp.float32)  92.8 us
    all_gather x1, waiting for transfers between devices, body(): lax.all_gather(factors.reshape(rows_all, rows_loc, state_cols), 'col', ax...  79.8 us
    unnamed x24, local copies, waits for them, and re-layouts  77.5 us
    dynamic_slice x32, local copies, waits for them, and re-layouts, body(): lax.scan(advance, (start_spikes, zeros, zeros, trace_zero), external)  44.8 us
  transfers between devices with their start and end apart: 18, of which 18 were waited for; matrix products, arithmetic and copies ran while one was open for 5% of the time, Pallas kernels for 0%

commit v1 on v0

--- a/solution.py
+++ b/solution.py
@@ -66,8 +66,11 @@
     )
     readout_loc = own_part(w_out, 1).reshape(rows_loc * own_cols, -1)
     projected = lax.psum(
-        jnp.dot(spikes.reshape(rows_all, -1), readout_loc, preferred_element_type=jnp.float32),
-        ("row", "col"),
+        lax.psum(
+            jnp.dot(spikes.reshape(rows_all, -1), readout_loc, preferred_element_type=jnp.float32),
+            "col",
+        ),
+        "row",
     )
     outputs_n = readout_loc.shape[1]
     projected = projected.reshape(steps_count, batch, outputs_n)

time: 1120 us -> 1080 us (0.964)
  waiting for transfers between devices: 570 us -> 534 us
    psum x1, waiting for transfers between devices: 129 us -> 37.1 us  [body(): lax.psum(jnp.dot(spikes.reshape(rows_all, -1), readout_loc, preferred_ele...]
    psum x0 -> x1, waiting for transfers between devices: none -> 56.2 us  [body(): lax.psum(lax.psum(jnp.dot(spikes.reshape(rows_all, -1), readout_loc, pref...]
  transfers between devices with their start and end apart: 18 -> 19, of which waited for: 18 -> 19; matrix products, arithmetic and copies ran while one was open for 5% -> 5% of each run, Pallas kernels for 0% -> 0%
where the time goes in v1:
time: 1080 us
  waiting for transfers between devices  534 us (49%)
  local copies, waits for them, and re-layouts  279 us (26%)
  matrix products  122 us (11%)
  other arithmetic  87.2 us (8%)
  blocking collectives  39.1 us (4%)
  between operations  16.3 us (2%)
    all_gather x8, waiting for transfers between devices, advance(): lax.all_gather(pulse_output, 'row', axis=1, tiled=True).reshape(batch, -1)  194 us
    reduce_scatter x8, waiting for transfers between devices, combine_currents(): lax.psum_scatter(partial_value, 'col', scatter_dimension=2, tiled=True)  166 us
    dynamic_update_slice x40, local copies, waits for them, and re-layouts, body(): lax.scan(advance, (start_spikes, zeros, zeros, trace_zero), external)  140 us
    dot_general x8, matrix products, advance(): jnp.dot(arrivals, weights, preferred_element_type=jnp.float32)  92.8 us
    all_gather x1, waiting for transfers between devices, body(): lax.all_gather(factors.reshape(rows_all, rows_loc, state_cols), 'col', ax...  80.1 us
    unnamed x24, local copies, waits for them, and re-layouts  77.5 us
    psum x1, waiting for transfers between devices, body(): lax.psum(lax.psum(jnp.dot(spikes.reshape(rows_all, -1), readout_loc, pref...  56.2 us
    dynamic_slice x32, local copies, waits for them, and re-layouts, body(): lax.scan(advance, (start_spikes, zeros, zeros, trace_zero), external)  44.8 us
  transfers between devices with their start and end apart: 19, of which 19 were waited for; matrix products, arithmetic and copies ran while one was open for 5% of the time, Pallas kernels for 0%

profile of v1, /device:TPU:0, one launch (start us, length us, event | category | flops | bytes accessed | tf_op | source)
XLA Modules:
  0.0 1078.6 jit_solution(14633883422737261854)
XLA Ops:
  15.9 17.2 %copy.96 = bf16[512,8,16,128]{3,1,2,0:T(8,128)(2,1)} copy(bf16[512,8,16,128]{3,2,1,0:T(8,128)(2,1)} %bitcast.115) | data formatting | bytes 33554432
  33.1 21.2 %copy.58 = bf16[4096,2048]{0,1:T(8,128)(2,1)} copy(bf16[4096,2048]{1,0:T(8,128)(2,1)} %bitcast.112) | data formatting | bytes 33554432
  55.9 592.0 %while.55 = (s32[]{:T(128)}, bf16[128,16,32]{0,2,1:T(8,128)(2,1)S(1)}, f32[128,16,32]{0,2,1:T(8,128)S(1)}, f32[128,16,32]{0,2,1:T(8,128)S(1)}, f32[128,4096]{0,1...) while((s32[]{:T(128)}, ...), condition=%wide.region_2.3_spmd.clone, body=%wide.region_0.2_spmd.clone.sunk | while | flops 2151677952 | bytes 45881672 | solution.py:64
  56.7 28.0 %all-gather.5.cloned.1.call-done = bf16[128,128,32]{0,2,1:T(8,128)(2,1)} async-done(((bf16[128,16,32]{0,2,1:T(8,128)(2,1)}), bf16[128,128,32]{0,2,1:T(8,128)(2,1)}) %all-gather.5.cloned.1.call-update) | async-done | bytes 1048592 | tf_op jit(solution)/shard_map/while/body/eval_jaxpr/all_gather | solution.py:43
  84.7 11.6 %fusion.29 = f32[128,16,128]{0,2,1:T(8,128)} fusion(bf16[128,4096,1]{0,1,2:T(8,128)(2,1)} %bitcast.111, bf16[16,128,4096]{2,1,0:T(8,128)(2,1)} %bitcast.109), kind=kOutput, calls=%fused_computation.43.clone.1 | convolution fusion | flops 2147483648 | bytes 18874368 | tf_op jit(solution)/shard_map/while/body/eval_jaxpr/dot_general | solution.py:45
  101.7 22.1 %reduce-scatter.2.cloned.1.call-done = f32[128,16,32]{0,2,1:T(8,128)} async-done(((f32[128,16,128]{0,2,1:T(8,128)}), f32[128,16,32]{0,2,1:T(8,128)}) %reduce-scatter.2.cloned.1.call-update) | async-done | bytes 262160 | tf_op jit(solution)/shard_map/while/body/eval_jaxpr/reduce_scatter | solution.py:27
  134.5 23.8 %all-gather.5.cloned.1.call-done = bf16[128,128,32]{0,2,1:T(8,128)(2,1)} async-done(((bf16[128,16,32]{0,2,1:T(8,128)(2,1)}), bf16[128,128,32]{0,2,1:T(8,128)(2,1)}) %all-gather.5.cloned.1.call-update) | async-done | bytes 1048592 | tf_op jit(solution)/shard_map/while/body/eval_jaxpr/all_gather | solution.py:43
  158.3 11.6 %fusion.29 = f32[128,16,128]{0,2,1:T(8,128)} fusion(bf16[128,4096,1]{0,1,2:T(8,128)(2,1)} %bitcast.111, bf16[16,128,4096]{2,1,0:T(8,128)(2,1)} %bitcast.109), kind=kOutput, calls=%fused_computation.43.clone.1 | convolution fusion | flops 2147483648 | bytes 18874368 | tf_op jit(solution)/shard_map/while/body/eval_jaxpr/dot_general | solution.py:45
  176.8 20.5 %reduce-scatter.2.cloned.1.call-done = f32[128,16,32]{0,2,1:T(8,128)} async-done(((f32[128,16,128]{0,2,1:T(8,128)}), f32[128,16,32]{0,2,1:T(8,128)}) %reduce-scatter.2.cloned.1.call-update) | async-done | bytes 262160 | tf_op jit(solution)/shard_map/while/body/eval_jaxpr/reduce_scatter | solution.py:27
  207.9 23.6 %all-gather.5.cloned.1.call-done = bf16[128,128,32]{0,2,1:T(8,128)(2,1)} async-done(((bf16[128,16,32]{0,2,1:T(8,128)(2,1)}), bf16[128,128,32]{0,2,1:T(8,128)(2,1)}) %all-gather.5.cloned.1.call-update) | async-done | bytes 1048592 | tf_op jit(solution)/shard_map/while/body/eval_jaxpr/all_gather | solution.py:43
  250.1 20.5 %reduce-scatter.2.cloned.1.call-done = f32[128,16,32]{0,2,1:T(8,128)} async-done(((f32[128,16,128]{0,2,1:T(8,128)}), f32[128,16,32]{0,2,1:T(8,128)}) %reduce-scatter.2.cloned.1.call-update) | async-done | bytes 262160 | tf_op jit(solution)/shard_map/while/body/eval_jaxpr/reduce_scatter | solution.py:27
  281.2 23.8 %all-gather.5.cloned.1.call-done = bf16[128,128,32]{0,2,1:T(8,128)(2,1)} async-done(((bf16[128,16,32]{0,2,1:T(8,128)(2,1)}), bf16[128,128,32]{0,2,1:T(8,128)(2,1)}) %all-gather.5.cloned.1.call-update) | async-done | bytes 1048592 | tf_op jit(solution)/shard_map/while/body/eval_jaxpr/all_gather | solution.py:43
  305.1 11.6 %fusion.29 = f32[128,16,128]{0,2,1:T(8,128)} fusion(bf16[128,4096,1]{0,1,2:T(8,128)(2,1)} %bitcast.111, bf16[16,128,4096]{2,1,0:T(8,128)(2,1)} %bitcast.109), kind=kOutput, calls=%fused_computation.43.clone.1 | convolution fusion | flops 2147483648 | bytes 18874368 | tf_op jit(solution)/shard_map/while/body/eval_jaxpr/dot_general | solution.py:45
  323.6 20.5 %reduce-scatter.2.cloned.1.call-done = f32[128,16,32]{0,2,1:T(8,128)} async-done(((f32[128,16,128]{0,2,1:T(8,128)}), f32[128,16,32]{0,2,1:T(8,128)}) %reduce-scatter.2.cloned.1.call-update) | async-done | bytes 262160 | tf_op jit(solution)/shard_map/while/body/eval_jaxpr/reduce_scatter | solution.py:27
  354.8 23.8 %all-gather.5.cloned.1.call-done = bf16[128,128,32]{0,2,1:T(8,128)(2,1)} async-done(((bf16[128,16,32]{0,2,1:T(8,128)(2,1)}), bf16[128,128,32]{0,2,1:T(8,128)(2,1)}) %all-gather.5.cloned.1.call-update) | async-done | bytes 1048592 | tf_op jit(solution)/shard_map/while/body/eval_jaxpr/all_gather | solution.py:43
  378.6 11.6 %fusion.29 = f32[128,16,128]{0,2,1:T(8,128)} fusion(bf16[128,4096,1]{0,1,2:T(8,128)(2,1)} %bitcast.111, bf16[16,128,4096]{2,1,0:T(8,128)(2,1)} %bitcast.109), kind=kOutput, calls=%fused_computation.43.clone.1 | convolution fusion | flops 2147483648 | bytes 18874368 | tf_op jit(solution)/shard_map/while/body/eval_jaxpr/dot_general | solution.py:45
  397.2 20.5 %reduce-scatter.2.cloned.1.call-done = f32[128,16,32]{0,2,1:T(8,128)} async-done(((f32[128,16,128]{0,2,1:T(8,128)}), f32[128,16,32]{0,2,1:T(8,128)}) %reduce-scatter.2.cloned.1.call-update) | async-done | bytes 262160 | tf_op jit(solution)/shard_map/while/body/eval_jaxpr/reduce_scatter | solution.py:27
  428.3 23.8 %all-gather.5.cloned.1.call-done = bf16[128,128,32]{0,2,1:T(8,128)(2,1)} async-done(((bf16[128,16,32]{0,2,1:T(8,128)(2,1)}), bf16[128,128,32]{0,2,1:T(8,128)(2,1)}) %all-gather.5.cloned.1.call-update) | async-done | bytes 1048592 | tf_op jit(solution)/shard_map/while/body/eval_jaxpr/all_gather | solution.py:43
  470.7 20.5 %reduce-scatter.2.cloned.1.call-done = f32[128,16,32]{0,2,1:T(8,128)} async-done(((f32[128,16,128]{0,2,1:T(8,128)}), f32[128,16,32]{0,2,1:T(8,128)}) %reduce-scatter.2.cloned.1.call-update) | async-done | bytes 262160 | tf_op jit(solution)/shard_map/while/body/eval_jaxpr/reduce_scatter | solution.py:27
  501.9 23.8 %all-gather.5.cloned.1.call-done = bf16[128,128,32]{0,2,1:T(8,128)(2,1)} async-done(((bf16[128,16,32]{0,2,1:T(8,128)(2,1)}), bf16[128,128,32]{0,2,1:T(8,128)(2,1)}) %all-gather.5.cloned.1.call-update) | async-done | bytes 1048592 | tf_op jit(solution)/shard_map/while/body/eval_jaxpr/all_gather | solution.py:43
  525.7 11.6 %fusion.29 = f32[128,16,128]{0,2,1:T(8,128)} fusion(bf16[128,4096,1]{0,1,2:T(8,128)(2,1)} %bitcast.111, bf16[16,128,4096]{2,1,0:T(8,128)(2,1)} %bitcast.109), kind=kOutput, calls=%fused_computation.43.clone.1 | convolution fusion | flops 2147483648 | bytes 18874368 | tf_op jit(solution)/shard_map/while/body/eval_jaxpr/dot_general | solution.py:45
  544.2 20.6 %reduce-scatter.2.cloned.1.call-done = f32[128,16,32]{0,2,1:T(8,128)} async-done(((f32[128,16,128]{0,2,1:T(8,128)}), f32[128,16,32]{0,2,1:T(8,128)}) %reduce-scatter.2.cloned.1.call-update) | async-done | bytes 262160 | tf_op jit(solution)/shard_map/while/body/eval_jaxpr/reduce_scatter | solution.py:27
  575.4 23.6 %all-gather.5.cloned.1.call-done = bf16[128,128,32]{0,2,1:T(8,128)(2,1)} async-done(((bf16[128,16,32]{0,2,1:T(8,128)(2,1)}), bf16[128,128,32]{0,2,1:T(8,128)(2,1)}) %all-gather.5.cloned.1.call-update) | async-done | bytes 1048592 | tf_op jit(solution)/shard_map/while/body/eval_jaxpr/all_gather | solution.py:43
  617.5 20.5 %reduce-scatter.2.cloned.1.call-done = f32[128,16,32]{0,2,1:T(8,128)} async-done(((f32[128,16,128]{0,2,1:T(8,128)}), f32[128,16,32]{0,2,1:T(8,128)}) %reduce-scatter.2.cloned.1.call-update) | async-done | bytes 262160 | tf_op jit(solution)/shard_map/while/body/eval_jaxpr/reduce_scatter | solution.py:27
  651.4 37.1 %all-reduce.3.cloned.1.call-done = f32[1024,128]{1,0:T(8,128)} async-done(((f32[1024,128]{1,0:T(8,128)}), f32[1024,128]{1,0:T(8,128)}) %all-reduce.3.cloned.1.call-update) | async-done | bytes 524304 | tf_op jit(solution)/shard_map/psum | solution.py:69
  689.1 56.2 %all-reduce.5.cloned.1.call-done = f32[8,128,128]{2,1,0:T(8,128)} async-done(((f32[8,128,128]{2,1,0:T(8,128)}), f32[8,128,128]{2,1,0:T(8,128)}) %all-reduce.5.cloned.1.call-update) | async-done | bytes 524304 | tf_op jit(solution)/shard_map/psum | solution.py:68
  762.3 112.8 %while.57 = (s32[]{:T(128)}, f32[128,16,32]{2,1,0:T(8,128)}, f32[8,128,16,32]{1,0,3,2:T(8,128)}, f32[8,128,16,32]{1,0,3,2:T(8,128)}, f32[8,128,16,32]{1,0,3,2:T(8,128)}, /*index=5*/s32[]{:T(128)}, s32[]{:T(128)}, s32[]{:T(128)}) while((s32[]{:T(128)}, f32[128,16,32]{2,1,0:T(8,128)}, f32[8,128,16,32]{1,0,3,2:T(8,128)}, ...), condition=%wide.region_8.9_spmd.clone, body=%wide.region_7.8_spmd.clone.sunk | while | flops 196612 | bytes 4456571 | solution.py:98
  879.6 80.1 %all-gather.3.cloned.1.call-done = bf16[1024,16,128]{0,2,1:T(8,128)(2,1)} async-done(((bf16[1024,16,32]{0,2,1:T(8,128)(2,1)}), bf16[1024,16,128]{0,2,1:T(8,128)(2,1)}) %all-gather.3.cloned.1.call-update) | async-done | bytes 4194320 | tf_op jit(solution)/shard_map/all_gather | solution.py:101
  959.7 26.1 %multiply_reduce_fusion = (f32[]{:T(128)}, f32[4096,16,128]{2,0,1:T(8,128)}) fusion(bf16[1024,4096,1]{1,0,2:T(8,128)(2,1)} %bitcast.128, bf16[1024,16,128]{0,2,1:T(8,128)(2,1)} %all-gather.3.cloned.1.call-done), kind=kOutput, calls=%fused_computation.22 | convolution fusion | flops 17196646400 | bytes 46137348 | tf_op jit(solution)/shard_map/dot_general | solution.py:104
  985.9 39.1 %psum.23 = f32[]{:T(128)} all-reduce(f32[]{:T(128)} %get-tuple-element.484), channel_id=1, replica_groups=mesh['row'=8,'col'=4] {'row','col'}, use_global_device_ids=true, to_apply=%region_10.11 | all-reduce | flops 1 | bytes 8 | tf_op jit(solution)/shard_map/psum | solution.py:111
  1025.6 11.9 %broadcast_multiply_fusion = f32[4096,16,128]{2,0,1:T(8,128)S(1)} fusion(f32[4096,16,128]{2,0,1:T(8,128)} %get-tuple-element.485, f32[]{:T(128)S(6)} %min.3), kind=kLoop, calls=%fused_computation.24 | loop fusion | flops 8388608 | bytes 67108864 | tf_op jit(solution)/shard_map/mul | solution.py:113
  1037.5 33.7 %copy.69 = f32[128,32,16,128]{3,2,1,0:T(8,128)} copy(f32[128,32,16,128]{3,1,0,2:T(8,128)S(1)} %bitcast.110) | data formatting | bytes 67108864
  (249 shorter events, 327.8 us)
Async XLA Ops:
  8.0 2.8 copy-start
  33.1 21.2 %copy-start.9 = (f32[16,128]{1,0:T(8,128)S(1)}, f32[16,128]{1,0:T(8,128)}, u32[]{:S(2)}) copy-start(f32[16,128]{1,0:T(8,128)} %param.23) | copy-start | bytes 24580
  33.1 21.2 %copy-start.10 = (f32[16,128]{1,0:T(8,128)S(1)}, f32[16,128]{1,0:T(8,128)}, u32[]{:S(2)}) copy-start(f32[16,128]{1,0:T(8,128)} %param.22) | copy-start | bytes 24580
  55.9 28.8 %all-gather.5.cloned.1.call-start = ((), (), s32[]{:S(2)}) async-start(), calls=%async_computation.4 | async-start | bytes 1179648 | tf_op jit(solution)/shard_map/while/body/eval_jaxpr/all_gather | solution.py:43
  56.6 67.2 %reduce-scatter.2.cloned.1.call-start = ((), (), s32[]{:S(2)}) async-start(), calls=%async_computation.5 | async-start | bytes 1310720 | tf_op jit(solution)/shard_map/while/body/eval_jaxpr/reduce_scatter | solution.py:27
  100.1 23.7 %copy-start.5 = (bf16[128,16,32]{0,2,1:T(8,128)(2,1)S(1)}, bf16[128,16,32]{0,2,1:T(8,128)(2,1)}, u32[]{:S(2)}) copy-start(bf16[128,16,32]{0,2,1:T(8,128)(2,1)} %copy-done.4) | copy-start | bytes 393220 | tf_op jit(solution)/shard_map/while
  133.7 24.6 %all-gather.5.cloned.1.call-start = ((), (), s32[]{:S(2)}) async-start(), calls=%async_computation.4 | async-start | bytes 1179648 | tf_op jit(solution)/shard_map/while/body/eval_jaxpr/all_gather | solution.py:43
  134.4 62.9 %reduce-scatter.2.cloned.1.call-start = ((), (), s32[]{:S(2)}) async-start(), calls=%async_computation.5 | async-start | bytes 1310720 | tf_op jit(solution)/shard_map/while/body/eval_jaxpr/reduce_scatter | solution.py:27
  175.2 22.2 %copy-start.5 = (bf16[128,16,32]{0,2,1:T(8,128)(2,1)S(1)}, bf16[128,16,32]{0,2,1:T(8,128)(2,1)}, u32[]{:S(2)}) copy-start(bf16[128,16,32]{0,2,1:T(8,128)(2,1)} %copy-done.4) | copy-start | bytes 393220 | tf_op jit(solution)/shard_map/while
  207.2 24.3 %all-gather.5.cloned.1.call-start = ((), (), s32[]{:S(2)}) async-start(), calls=%async_computation.4 | async-start | bytes 1179648 | tf_op jit(solution)/shard_map/while/body/eval_jaxpr/all_gather | solution.py:43
  207.9 62.7 %reduce-scatter.2.cloned.1.call-start = ((), (), s32[]{:S(2)}) async-start(), calls=%async_computation.5 | async-start | bytes 1310720 | tf_op jit(solution)/shard_map/while/body/eval_jaxpr/reduce_scatter | solution.py:27
  248.4 22.2 %copy-start.5 = (bf16[128,16,32]{0,2,1:T(8,128)(2,1)S(1)}, bf16[128,16,32]{0,2,1:T(8,128)(2,1)}, u32[]{:S(2)}) copy-start(bf16[128,16,32]{0,2,1:T(8,128)(2,1)} %copy-done.4) | copy-start | bytes 393220 | tf_op jit(solution)/shard_map/while
  280.5 24.6 %all-gather.5.cloned.1.call-start = ((), (), s32[]{:S(2)}) async-start(), calls=%async_computation.4 | async-start | bytes 1179648 | tf_op jit(solution)/shard_map/while/body/eval_jaxpr/all_gather | solution.py:43
  281.2 62.9 %reduce-scatter.2.cloned.1.call-start = ((), (), s32[]{:S(2)}) async-start(), calls=%async_computation.5 | async-start | bytes 1310720 | tf_op jit(solution)/shard_map/while/body/eval_jaxpr/reduce_scatter | solution.py:27
  322.0 22.2 %copy-start.5 = (bf16[128,16,32]{0,2,1:T(8,128)(2,1)S(1)}, bf16[128,16,32]{0,2,1:T(8,128)(2,1)}, u32[]{:S(2)}) copy-start(bf16[128,16,32]{0,2,1:T(8,128)(2,1)} %copy-done.4) | copy-start | bytes 393220 | tf_op jit(solution)/shard_map/while
  354.0 24.6 %all-gather.5.cloned.1.call-start = ((), (), s32[]{:S(2)}) async-start(), calls=%async_computation.4 | async-start | bytes 1179648 | tf_op jit(solution)/shard_map/while/body/eval_jaxpr/all_gather | solution.py:43
  354.7 62.9 %reduce-scatter.2.cloned.1.call-start = ((), (), s32[]{:S(2)}) async-start(), calls=%async_computation.5 | async-start | bytes 1310720 | tf_op jit(solution)/shard_map/while/body/eval_jaxpr/reduce_scatter | solution.py:27
  395.5 22.2 %copy-start.5 = (bf16[128,16,32]{0,2,1:T(8,128)(2,1)S(1)}, bf16[128,16,32]{0,2,1:T(8,128)(2,1)}, u32[]{:S(2)}) copy-start(bf16[128,16,32]{0,2,1:T(8,128)(2,1)} %copy-done.4) | copy-start | bytes 393220 | tf_op jit(solution)/shard_map/while
  427.6 24.6 %all-gather.5.cloned.1.call-start = ((), (), s32[]{:S(2)}) async-start(), calls=%async_computation.4 | async-start | bytes 1179648 | tf_op jit(solution)/shard_map/while/body/eval_jaxpr/all_gather | solution.py:43
  428.3 62.9 %reduce-scatter.2.cloned.1.call-start = ((), (), s32[]{:S(2)}) async-start(), calls=%async_computation.5 | async-start | bytes 1310720 | tf_op jit(solution)/shard_map/while/body/eval_jaxpr/reduce_scatter | solution.py:27
  469.1 22.2 %copy-start.5 = (bf16[128,16,32]{0,2,1:T(8,128)(2,1)S(1)}, bf16[128,16,32]{0,2,1:T(8,128)(2,1)}, u32[]{:S(2)}) copy-start(bf16[128,16,32]{0,2,1:T(8,128)(2,1)} %copy-done.4) | copy-start | bytes 393220 | tf_op jit(solution)/shard_map/while
  501.1 24.6 %all-gather.5.cloned.1.call-start = ((), (), s32[]{:S(2)}) async-start(), calls=%async_computation.4 | async-start | bytes 1179648 | tf_op jit(solution)/shard_map/while/body/eval_jaxpr/all_gather | solution.py:43
  501.8 62.9 %reduce-scatter.2.cloned.1.call-start = ((), (), s32[]{:S(2)}) async-start(), calls=%async_computation.5 | async-start | bytes 1310720 | tf_op jit(solution)/shard_map/while/body/eval_jaxpr/reduce_scatter | solution.py:27
  542.6 22.2 %copy-start.5 = (bf16[128,16,32]{0,2,1:T(8,128)(2,1)S(1)}, bf16[128,16,32]{0,2,1:T(8,128)(2,1)}, u32[]{:S(2)}) copy-start(bf16[128,16,32]{0,2,1:T(8,128)(2,1)} %copy-done.4) | copy-start | bytes 393220 | tf_op jit(solution)/shard_map/while
  574.7 24.3 %all-gather.5.cloned.1.call-start = ((), (), s32[]{:S(2)}) async-start(), calls=%async_computation.4 | async-start | bytes 1179648 | tf_op jit(solution)/shard_map/while/body/eval_jaxpr/all_gather | solution.py:43
  575.3 62.7 %reduce-scatter.2.cloned.1.call-start = ((), (), s32[]{:S(2)}) async-start(), calls=%async_computation.5 | async-start | bytes 1310720 | tf_op jit(solution)/shard_map/while/body/eval_jaxpr/reduce_scatter | solution.py:27
  615.9 22.2 %copy-start.5 = (bf16[128,16,32]{0,2,1:T(8,128)(2,1)S(1)}, bf16[128,16,32]{0,2,1:T(8,128)(2,1)}, u32[]{:S(2)}) copy-start(bf16[128,16,32]{0,2,1:T(8,128)(2,1)} %copy-done.4) | copy-start | bytes 393220 | tf_op jit(solution)/shard_map/while
  647.9 40.6 %all-reduce.3.cloned.1.call-start = ((), (), s32[]{:S(2)}) async-start(), calls=%async_computation.1 | async-start | bytes 1048576 | tf_op jit(solution)/shard_map/psum | solution.py:69
  649.8 102.6 %copy-start.6 = (s32[8,128,128]{2,1,0:T(8,128)S(1)}, s32[8,128,128]{2,1,0:T(8,128)}, u32[]{:S(2)}) copy-start(s32[8,128,128]{2,1,0:T(8,128)} %param.16) | copy-start | bytes 1572868
  651.2 94.1 %all-reduce.5.cloned.1.call-start = ((), (), s32[]{:S(2)}) async-start(), calls=%async_computation.2 | async-start | bytes 1048576 | tf_op jit(solution)/shard_map/psum | solution.py:68
  688.5 271.2 %all-gather.3.cloned.1.call-start = ((), (), s32[]{:S(2)}) async-start(), calls=%async_computation.3 | async-start | bytes 5242880 | tf_op jit(solution)/shard_map/all_gather | solution.py:101
  1037.5 33.7 %copy-start.1 = (s32[128,16,128]{2,1,0:T(8,128)S(1)}, s32[128,16,128]{2,1,0:T(8,128)}, u32[]{:S(2)}) copy-start(s32[128,16,128]{2,1,0:T(8,128)} %param.17) | copy-start | bytes 3145732
  (19 other events, 26.0 us)
Sparse Core Ops, SparseCore 0:
  58.6 26.0 all-gather.4
  96.5 27.2 reduce-scatter.1
  136.4 21.8 all-gather.4
  170.0 27.2 reduce-scatter.1
  209.6 21.8 all-gather.4
  243.3 27.2 reduce-scatter.1
  283.1 21.8 all-gather.4
  316.8 27.2 reduce-scatter.1
  356.7 21.8 all-gather.4
  390.4 27.2 reduce-scatter.1
  430.2 21.8 all-gather.4
  463.9 27.2 reduce-scatter.1
  503.8 21.8 all-gather.4
  537.5 27.2 reduce-scatter.1
  577.0 21.8 all-gather.4
  610.7 27.2 reduce-scatter.1
Sparse Core Ops, SparseCore 1:
  651.3 37.2 all-reduce.2
  691.5 53.8 all-reduce.4
  879.7 80.0 all-gather.2
